TPU v7x, 256 devices: a whole 4x4x8 slice. The times are simulated.
256 devices in a mesh: tm: 2 (over y_lo), row: 16 (over y_hi, z), col: 8 (over x, core).
Axes of the slice: x: 4, y: 4 (y_hi: 2, y_lo: 2; y = y_hi * 2 + y_lo), z: 8, core: 2. Of those that a mesh axis runs over, the one named last changes fastest.
Arguments:
- returns: bfloat16 [272, 16384], P('tm', ('row', 'col')), may hold values from -60 to 60
- window: int32 [1], replicated, may hold values from 200 to 256
- out_days: int32 [4], replicated, may hold values from 255 to 271
Outputs:
- correlation: bfloat16 [4, 16384, 16384], P(None, 'row', ('col', 'tm'))
Inputs may be any that keep to these rules, and one draw needn't show every extreme that they name: One window length for all days. `out_days`: days may repeat.
All inputs are finite; a program needn't handle non-finite values.
Results may differ from a plain program's by a relative error of at most 0.001.
Values may be sent and summed in bfloat16 or wider, within the bound.
No kernel may reach another device: no remote copies, remote signals or barrier semaphores. Data moves between devices by JAX's collectives and lax.ppermute only.
A program may use at most 128 MiB of HBM per device.

v0:
```python
import jax
import jax.numpy as jnp
from jax import lax
from jax.sharding import PartitionSpec as P


def moments(mask, block):
    series = block.astype(jnp.float32)
    first = jnp.dot(mask, series, precision=lax.Precision.HIGHEST)
    second = jnp.dot(mask, series * series, precision=lax.Precision.HIGHEST)
    return (first, second)


def on_device(returns, window, out_days):
    width = window[0]
    wide = width.astype(jnp.float32)
    tm_count = lax.axis_size("tm")
    tm_index = lax.axis_index("tm")
    share = lax.axis_size("row") // lax.axis_size("col")
    local = lax.all_gather(returns, "tm", axis=0, tiled=True)
    row_series = lax.all_gather(local, "col", axis=1, tiled=True)
    block_width = row_series.shape[1]
    col_index = lax.axis_index("col")
    range_width = share * block_width
    half = range_width // tm_count
    half_start = tm_index * half
    range_start = col_index * range_width
    wanted_start = range_start + half_start
    everything = lax.all_gather(row_series, "row", axis=1, tiled=True)
    col_series = lax.dynamic_slice_in_dim(everything, wanted_start, half, 1)
    day_count = local.shape[0]
    day_ids = jnp.arange(day_count, dtype=jnp.int32)
    inside = (day_ids[None, :] <= out_days[:, None]) & (
        day_ids[None, :] > out_days[:, None] - width
    )
    mask = jnp.where(inside, 1.0, 0.0).astype(jnp.float32)
    weighted = mask.astype(jnp.bfloat16)[:, :, None] * row_series[None, :, :]
    gram = jnp.einsum("kda,db->kab", weighted, col_series, preferred_element_type=jnp.float32)
    first_rows, second_rows = moments(mask, row_series)
    first_cols, second_cols = moments(mask, col_series)
    scale_rows = lax.rsqrt((second_rows - first_rows * first_rows / wide) / wide + 1e-06)
    scale_cols = lax.rsqrt((second_cols - first_cols * first_cols / wide) / wide + 1e-06)
    cov = gram - first_rows[:, :, None] * first_cols[:, None, :] / wide
    return (cov * scale_rows[:, :, None] * scale_cols[:, None, :] / wide).astype(jnp.bfloat16)


def solution(mesh):
    return jax.shard_map(
        on_device,
        mesh=mesh,
        in_specs=(P("tm", ("row", "col")), P(), P()),
        out_specs=P(None, "row", ("col", "tm")),
        check_vma=False,
    )
```

profile of v0, /device:TPU:1, one launch (start us, length us, event | category | flops | bytes accessed | tf_op | source)
XLA Modules:
  0.0 188.0 jit_solution(15276482759653825243)
XLA Ops:
  6.5 0.0 all-gather.2.cloned.1.call-start
  6.5 4.4 %all_gather.9 = bf16[272,128]{1,0:T(8,128)(2,1)S(1)} all-gather(bf16[136,128]{1,0:T(8,128)(2,1)} %param.3), channel_id=1, replica_groups=mesh['tm'=2,'row'=16,'col'=8] {'tm'}, dimensions={0}, use_global_device_ids=true | all-gather | bytes 104448 | tf_op jit(solution)/shard_map/all_gather | solution.py:20
  10.9 16.4 %all_gather.10 = bf16[272,1024]{1,0:T(8,128)(2,1)} all-gather(bf16[272,128]{1,0:T(8,128)(2,1)S(1)} %all_gather.9), channel_id=1, replica_groups=mesh['tm'=2,'row'=16,'col'=8] {'col'}, dimensions={1}, use_global_device_ids=true | all-gather | bytes 626688 | tf_op jit(solution)/shard_map/all_gather | solution.py:21
  27.3 0.0 all-gather.2.cloned.1.call-update
  28.0 0.7 broadcast_subtract_fusion
  28.7 0.7 select_convert_fusion
  29.4 1.4 fusion.41
  30.8 1.8 fusion.18
  32.7 135.3 %all-gather.2.cloned.1.call-done = bf16[272,16384]{1,0:T(8,128)(2,1)} async-done(((bf16[272,1024]{1,0:T(8,128)(2,1)}), bf16[272,16384]{1,0:T(8,128)(2,1)}) %all-gather.2.cloned.1.call-update) | async-done | bytes 8912912 | tf_op jit(solution)/shard_map/all_gather | solution.py:29
  168.0 1.4 fusion.35
  169.4 1.8 fusion.30
  171.2 9.9 %divide_convert_fusion = bf16[4,1024,1024]{2,1,0:T(8,128)(2,1)} fusion(f32[4,1024]{1,0:T(4,128)S(1)} %fusion.30, f32[4,1024]{1,0:T(4,128)S(1)} %fusion.18, f32[]{:T(128)S(6)} %convert_element_type.20, f32[4,1024]{1,0:T(4,128)S(1)} %fusion.35, f32[4,1024]{1,0:T(4,128)S(1)} %fusion.41, bf16[272,1024]{1,0:T(8,128)(2,1)} %all_gather.10, ...), kind=kOutput, calls=%fused_computation | convolution fusion | flops 2312175616 | bytes 9570440 | tf_op jit(solution)/shard_map/kda,db->kab/dot_general | solution.py:38
Async XLA Ops:
  6.5 161.4 %all-gather.2.cloned.1.call-start = ((), (), s32[]{:S(2)}) async-start(), calls=%async_computation | async-start | bytes 9469952 | tf_op jit(solution)/shard_map/all_gather | solution.py:29
Sparse Core Ops, SparseCore 0:
  27.5 140.4 all-gather.1
where the time goes:
time: 188 us
  waiting for transfers between devices  135 us (72%)
  blocking collectives  20.8 us (11%)
  matrix products  16.4 us (9%)
  between operations  14.1 us (8%)
    all_gather x1, waiting for transfers between devices, on_device(): everything = lax.all_gather(row_series, 'row', axis=1, tiled=True)  135 us
    all_gather x1, blocking collectives, on_device(): row_series = lax.all_gather(local, 'col', axis=1, tiled=True)  16.4 us
    dot_general x1, matrix products, on_device(): jnp.einsum('kda,db->kab', weighted, col_series, preferred_element_type=jn...  9.89 us
    all_gather x1, blocking collectives, on_device(): local = lax.all_gather(returns, 'tm', axis=0, tiled=True)  4.36 us
  transfers between devices with their start and end apart: 1, of which 1 were waited for; matrix products, arithmetic and copies ran while one was open for 2% of the time, Pallas kernels for 0%

commit v1 on v0

--- a/solution.py
+++ b/solution.py
@@ -26,7 +26,8 @@
     half_start = tm_index * half
     range_start = col_index * range_width
     wanted_start = range_start + half_start
-    everything = lax.all_gather(row_series, "row", axis=1, tiled=True)
+    pieces = lax.all_gather(row_series, "row")
+    everything = jnp.concatenate(pieces, axis=1)
     col_series = lax.dynamic_slice_in_dim(everything, wanted_start, half, 1)
     day_count = local.shape[0]
     day_ids = jnp.arange(day_count, dtype=jnp.int32)

time: 188 us -> 197 us (1.048)
  local copies, waits for them, and re-layouts: 0 us -> 8.58 us
    unnamed x0 -> x5, local copies, waits for them, and re-layouts: none -> 8.58 us
where the time goes in v1:
time: 197 us; the launch traced here: 196 us
  waiting for transfers between devices  135 us (69%)
  blocking collectives  20.8 us (11%)
  matrix products  16.3 us (8%)
  between operations  14.1 us (7%)
  local copies, waits for them, and re-layouts  8.58 us (4%)
    all_gather x1, waiting for transfers between devices, on_device(): pieces = lax.all_gather(row_series, 'row')  135 us
    all_gather x1, blocking collectives, on_device(): row_series = lax.all_gather(local, 'col', axis=1, tiled=True)  16.4 us
    dot_general x1, matrix products, on_device(): jnp.einsum('kda,db->kab', weighted, col_series, preferred_element_type=jn...  9.74 us
    unnamed x5, local copies, waits for them, and re-layouts  8.58 us
    all_gather x1, blocking collectives, on_device(): local = lax.all_gather(returns, 'tm', axis=0, tiled=True)  4.36 us
  transfers between devices with their start and end apart: 1, of which 1 were waited for; matrix products, arithmetic and copies ran while one was open for 2% of the time, Pallas kernels for 0%

profile of v1, /device:TPU:1, one launch (start us, length us, event | category | flops | bytes accessed | tf_op | source)
XLA Modules:
  0.0 196.4 jit_solution(16643541785082876352)
XLA Ops:
  6.5 0.0 all-gather.3.cloned.1.call-start
  6.5 4.4 %all_gather.10 = bf16[272,128]{1,0:T(8,128)(2,1)S(1)} all-gather(bf16[136,128]{1,0:T(8,128)(2,1)} %param.3), channel_id=1, replica_groups=mesh['tm'=2,'row'=16,'col'=8] {'tm'}, dimensions={0}, use_global_device_ids=true | all-gather | bytes 104448 | tf_op jit(solution)/shard_map/all_gather | solution.py:20
  10.9 16.4 %all_gather.11 = bf16[272,1024]{1,0:T(8,128)(2,1)} all-gather(bf16[272,128]{1,0:T(8,128)(2,1)S(1)} %all_gather.10), channel_id=1, replica_groups=mesh['tm'=2,'row'=16,'col'=8] {'col'}, dimensions={1}, use_global_device_ids=true | all-gather | bytes 626688 | tf_op jit(solution)/shard_map/all_gather | solution.py:21
  27.3 0.0 all-gather.3.cloned.1.call-update
  28.0 0.7 broadcast_subtract_fusion
  28.7 0.7 select_convert_fusion
  29.4 1.4 fusion.41
  30.8 1.8 fusion.18
  32.7 135.3 %all-gather.3.cloned.1.call-done = bf16[4352,1024]{1,0:T(8,128)(2,1)} async-done(((bf16[272,1024]{1,0:T(8,128)(2,1)}), bf16[4352,1024]{1,0:T(8,128)(2,1)}) %all-gather.3.cloned.1.call-update) | async-done | bytes 8912912 | tf_op jit(solution)/shard_map/all_gather | solution.py:29
  168.0 0.0 copy-start.1
  168.0 0.0 copy-start
  168.0 8.6 %copy.5 = bf16[34,8,16,1024]{3,1,2,0:T(8,128)(2,1)} copy(bf16[34,8,16,1024]{3,1,0,2:T(8,128)(2,1)} %bitcast.16) | data formatting | bytes 17825792
  176.5 0.0 copy-done.1
  176.5 1.4 fusion.35
  178.0 1.8 fusion.30
  179.8 0.0 copy-done
  179.8 9.7 %divide_convert_fusion = bf16[4,1024,1024]{2,1,0:T(8,128)(2,1)} fusion(f32[4,1024]{1,0:T(4,128)S(1)} %fusion.30, f32[4,1024]{1,0:T(4,128)S(1)} %fusion.18, f32[]{:T(128)S(6)} %convert_element_type.20, f32[4,1024]{1,0:T(4,128)S(1)} %fusion.35, f32[4,1024]{1,0:T(4,128)S(1)} %fusion.41, bf16[272,1024]{1,0:T(8,128)(2,1)S(1)} %copy-done, ...), kind=kOutput, calls=%fused_computation | convolution fusion | flops 2312175616 | bytes 9570440 | tf_op jit(solution)/shard_map/kda,db->kab/dot_general | solution.py:39
Async XLA Ops:
  6.5 161.4 %all-gather.3.cloned.1.call-start = ((), (), s32[]{:S(2)}) async-start(), calls=%async_computation | async-start | bytes 9469952 | tf_op jit(solution)/shard_map/all_gather | solution.py:29
  168.0 8.6 %copy-start.1 = (s32[4]{0:T(128)S(1)}, s32[4]{0:T(128)}, u32[]{:S(2)}) copy-start(s32[4]{0:T(128)} %param.5) | copy-start | bytes 52
  168.0 11.8 %copy-start = (bf16[272,1024]{1,0:T(8,128)(2,1)S(1)}, bf16[272,1024]{1,0:T(8,128)(2,1)}, u32[]{:S(2)}) copy-start(bf16[272,1024]{1,0:T(8,128)(2,1)} %all_gather.11) | copy-start | bytes 1671172
Sparse Core Ops, SparseCore 0:
  27.5 140.4 all-gather.2
